TPU v7x, 32 devices: a whole 2x2x4 slice. The times are simulated.
32 devices in a mesh: node: 8 (over y, x, core), stripe: 4 (over z).
Axes of the slice: x: 2, y: 2, z: 4, core: 2. Of those that a mesh axis runs over, the one named last changes fastest.
Arguments:
- groups: bfloat16 [4, 16, 256, 8, 512], P('stripe', 'node'), may hold values from -21 to 21
- gamma: float32 [8, 8], replicated, may hold values from -2 to 2
- coeffs: float32 [4, 12, 8, 8], replicated, may hold values from -0.625 to 0.625
Outputs:
- syndrome: float32 [256, 4, 4, 8, 512], P('node', 'stripe')
- scores: float32 [256, 4, 4], P('node', 'stripe')
All inputs are finite; a program needn't handle non-finite values.
Results may differ from a plain program's by a relative error of at most 0.0003.
Values may be sent and summed in bfloat16 or wider, within the bound.
No kernel may reach another device: no remote copies, remote signals or barrier semaphores. Data moves between devices by JAX's collectives and lax.ppermute only.
A program may use at most 64 MiB of HBM per device.

v0:
```python
import jax
import jax.numpy as jnp
from jax import lax
from jax.sharding import PartitionSpec as P

LAYERS = 256
PLANES = 8
PARITY = 4
DATA_NODES = 12
VIRTUAL = 2
precise = lax.Precision.HIGHEST
epsilon = 1e-06


def for_sending(x):
    return jax.tree.map(lambda a: a.astype(jnp.bfloat16) if a.dtype == jnp.float32 else a, x)


def from_behind(block, axis, distance):
    devices = range(lax.axis_size(axis))
    route = [((i - distance) % len(devices), i) for i in devices]
    return lax.ppermute(block, axis, route)


def mix_planes(matrix, values):
    return jnp.einsum("pq,...qb->...pb", matrix, values, precision=precise)


def inverse_factor(gamma):
    order_count = gamma.shape[0]
    identity = jnp.eye(order_count, dtype=jnp.float32)
    mixed = identity + jnp.dot(gamma.T, gamma, precision=precise)
    factor = jnp.linalg.cholesky(mixed)
    solved_rows = []
    for row_at in range(order_count):
        running = identity[row_at]
        for earlier in range(row_at):
            running = running - factor[row_at, earlier] * solved_rows[earlier]
        solved_rows.append(running / factor[row_at, row_at])
    solved = jnp.stack(solved_rows)
    return jnp.dot(solved.T, solved, precision=precise)


def to_front(values, digit_axis):

    def to_mover(position):
        return lambda operand: jnp.moveaxis(operand, 4 - position, 1)

    return lax.switch(digit_axis, [to_mover(position) for position in range(4)], values)


def from_front(values, digit_axis):

    def from_mover(position):
        return lambda operand: jnp.moveaxis(operand, 1, 4 - position)

    return lax.switch(digit_axis, [from_mover(position) for position in range(4)], values)


def local(groups, gamma, coeffs):
    stripes_here = groups.shape[0]
    nodes_here = groups.shape[1]
    byte_count = groups.shape[4]
    device = lax.axis_index("node")
    first_node = device * nodes_here
    column = first_node // 4
    inverse = inverse_factor(gamma)
    node_ids = first_node + jnp.arange(nodes_here)
    keep_mask = ((node_ids < DATA_NODES - VIRTUAL) | (node_ids >= DATA_NODES)).astype(jnp.bfloat16)
    stored = groups * keep_mask[None, :, None, None, None]
    fronts = []
    for local_node in range(nodes_here):
        row_index = (first_node + local_node) % 4
        layer_grid = stored[:, local_node].reshape(stripes_here, 4, 4, 4, 4, PLANES, byte_count)
        fronts.append(
            to_front(layer_grid, row_index).reshape(
                stripes_here, 4, LAYERS // 4, PLANES, byte_count
            )
        )
    fronted = jnp.stack(fronts, axis=1)
    step_nodes = 4 // nodes_here
    received = []
    for offset in range(1, 4):
        partner_piece = from_behind(
            for_sending(
                lax.dynamic_index_in_dim(fronted, (column + offset) % 4, axis=2, keepdims=False)
            ),
            "node",
            offset * step_nodes,
        )
        received.append(((column - offset) % 4, partner_piece))
    own_front = fronted.astype(jnp.float32)
    result = own_front
    for slot_index, partner_piece in received:
        own_rows = lax.dynamic_index_in_dim(own_front, slot_index, axis=2, keepdims=False)
        theirs = partner_piece.astype(jnp.float32)
        own_lower = column < slot_index
        lower_rows = jnp.where(own_lower, own_rows, theirs)
        upper_rows = jnp.where(own_lower, theirs, own_rows)
        upper_part = mix_planes(inverse, upper_rows + mix_planes(gamma.T, lower_rows))
        values = jnp.where(own_lower, lower_rows - mix_planes(gamma, upper_part), upper_part)
        result = lax.dynamic_update_index_in_dim(result, values, slot_index, axis=2)
    backs = []
    for local_node in range(nodes_here):
        row_index = (first_node + local_node) % 4
        layer_grid = result[:, local_node].reshape(stripes_here, 4, 4, 4, 4, PLANES, byte_count)
        backs.append(
            from_front(layer_grid, row_index).reshape(stripes_here, LAYERS, PLANES, byte_count)
        )
    uncoupled = jnp.stack(backs, axis=1)
    identity = jnp.eye(PLANES, dtype=jnp.float32)
    blocks = jnp.eye(PARITY, dtype=jnp.float32)[:, :, None, None] * identity[None, None]
    weights_all = jnp.concatenate([-coeffs, blocks], axis=1)
    syndrome = jnp.einsum(
        "ijpq,sjlqb->lsipb",
        weights_all,
        lax.all_to_all(uncoupled, "node", split_axis=2, concat_axis=1, tiled=True),
        precision=precise,
    )
    energy = jnp.mean(syndrome * syndrome, axis=(3, 4))
    pool_sum = lax.psum(jnp.sum(energy, axis=1), "stripe")
    stripe_total = stripes_here * lax.axis_size("stripe")
    scores = energy / (pool_sum[:, None, :] / stripe_total + epsilon)
    return (syndrome, scores)


def solution(mesh):
    return jax.shard_map(
        local,
        mesh=mesh,
        in_specs=(P("stripe", "node", None, None, None), P(), P()),
        out_specs=(P("node", "stripe", None, None, None), P("node", "stripe", None)),
        check_vma=False,
    )
```

profile of v0, /device:TPU:0, one launch (start us, length us, event | category | flops | bytes accessed | tf_op | source)
XLA Modules:
  0.0 257.2 jit_solution(47889790480864739)
XLA Ops:
  0.8 2.5 broadcast_multiply_fusion
  3.3 2.0 copy-done.3
  5.3 0.7 conditional.5
  5.3 0.1 slice.135
  5.5 0.2 copy.111
  5.7 0.3 copy.112
  6.1 1.3 copy-done.4
  7.4 3.1 %conditional.4 = (bf16[1,1,4,64,8,512]{5,4,2,3,1,0:T(8,128)(2,1)}) conditional(s32[]{:T(128)} %clamp.8, bf16[1,2,256,8,512]{4,3,2,1,0:T(8,128)(2,1)} %copy-done.3, bf16[1,2,256,8,512]{4,3,2,1,0:T(8,128)(2,1)} %copy-done.3, bf16[1,2,256,8,512]{4,3,2,1,0:T(8,128)(2,1)} %copy-done.3, ...), branch_computations={%region_0.1_spmd, %region_1.2_spmd, %region_2.3_spmd, %region_3.4_... | conditional | bytes 14680096 | solution.py:49
  7.4 3.1 %slice.130 = bf16[1,1,256,8,512]{4,3,2,1,0:T(8,128)(2,1)} slice(bf16[1,2,256,8,512]{4,3,2,1,0:T(8,128)(2,1)} %param), slice={[0:1], [0:1], [0:256], [0:8], [0:512]} | slice | bytes 4194304 | tf_op jit(solution)/shard_map/slice | solution.py:74
  10.4 6.8 %fusion.75 = (bf16[1,2,4,64,8,512]{5,4,3,2,1,0:T(8,128)(2,1)}, f32[1,2,4,64,8,512]{5,4,3,2,1,0:T(8,128)}) fusion(bf16[1,1,4,64,8,512]{5,4,2,3,1,0:T(8,128)(2,1)} %copy-done.4, bf16[1,1,4,64,8,512]{5,4,2,3,1,0:T(8,128)(2,1)} %get-tuple-element.139), kind=kLoop, calls=%fused_computation.104 | loop fusion | flops 4194304 | bytes 16777216 | tf_op jit(solution)/shard_map/stack | solution.py:80
  17.2 3.6 %dynamic-slice_bitcast_fusion = (bf16[1,2,64,8,512]{4,3,2,1,0:T(8,128)(2,1)}, bf16[1,2,64,8,512]{4,3,2,1,0:T(8,128)(2,1)}, bf16[1,2,64,8,512]{4,3,2,1,0:T(8,128)(2,1)}) fusion(bf16[1,2,4,64,8,512]{5,4,3,2,1,0:T(8,128)(2,1)} %get-tuple-element.99, s32[]{:T(128)S(6)} %select_n.139, s32[]{:T(128)S(6)} %select_n.131, s32[]{:T(128)S(6)} %select_n.122), kind=kLoop, calls=%fused_computation.54 | loop fusion | bytes 6291468 | tf_op jit(solution)/shard_map/jit(dynamic_index_in_dim)/squeeze | solution.py:86
  20.8 3.0 %collective-permute-start = (bf16[1,2,64,8,512]{4,3,2,1,0:T(8,128)(2,1)}, bf16[1,2,64,8,512]{4,3,2,1,0:T(8,128)(2,1)S(1)}, u32[]{:S(2)}, u32[]{:S(2)}) collective-permute-start(bf16[1,2,64,8,512]{4,3,2,1,0:T(8,128)(2,1)} %get-tuple-element.98), channel_id=1, source_target_pairs={{24,0},{28,4},{0,8},{4,12},{8,16},{12,20},{16,24},{20,28},{25,1},{... | collective-permute-start | bytes 3145736 | tf_op jit(solution)/shard_map/ppermute | solution.py:22
  23.8 1.5 collective-permute-start.1
  25.3 1.9 collective-permute-start.2
  27.2 0.2 fusion.78
  27.4 0.7 cholesky.14
  28.3 7.6 %copy.162 = f32[1,2,4,64,8,512]{5,4,3,2,1,0:T(8,128)} copy(f32[1,2,4,64,8,512]{5,4,3,2,1,0:T(8,128)} %get-tuple-element.100) | data formatting | bytes 16777216
  35.9 0.6 compare_reduce_fusion
  36.5 0.6 select_select_fusion
  37.0 0.7 fusion.77
  37.8 0.7 fusion.76
  38.5 22.5 %subtract_divide_fusion = (f32[1,8]{1,0:T(1,128)S(1)}, f32[1,8]{1,0:T(1,128)S(1)}, f32[1,8]{1,0:T(1,128)S(1)}, f32[1,8]{1,0:T(1,128)S(1)}, f32[1,8]{1,0:T(1,128)...) fusion(f32[8,8]{1,0:T(8,128)S(1)} %fusion.66, f32[]{:T(128)} %bitcast.83, f32[]{:T(128)} %bitcast.82, ...), kind=kLoop, calls=%fused_computation.94 | loop fusion | flops 512 | bytes 656 | tf_op jit(solution)/shard_map/div | solution.py:39
  61.0 0.2 convolution_bitcast_fusion
  61.2 2.1 convert_select_fusion.5
  63.3 2.0 fusion.33
  65.3 2.2 fusion.4
  67.5 3.2 %collective-permute-done.1 = bf16[1,2,64,8,512]{4,3,2,1,0:T(8,128)(2,1)S(1)} collective-permute-done((bf16[1,2,64,8,512]{4,3,2,1,0:T(8,128)(2,1)}, bf16[1,2,64,8,512]{4,3,2,1,0:T(8,128)(2,1)S(1)}, u32[]{:S(2)}, u32[]{:S(2)}) %collective-permute-start.1) | collective-permute-done | bytes 1048608 | tf_op jit(solution)/shard_map/ppermute | solution.py:22
  70.7 2.1 fusion.30
  72.8 2.2 fusion.8
  75.1 4.0 %bitcast_dynamic-update-slice_fusion.2 = f32[1,2,4,64,8,512]{5,4,3,2,1,0:T(8,128)} fusion(f32[1,2,4,64,8,512]{5,4,3,2,1,0:T(8,128)} %copy.162, s32[]{:T(128)S(6)} %select_n.120, f32[1,2,64,8,512]{4,3,2,1,0:T(8,128)S(1)} %convert_select_fusion.5, f32[2,64,512,8]{2,3,1,0:T(8,128)S(1)} %fusion.4, pred[]{:T(512)S(6)} %lt.82, f32[8,8]{1,0:T(8,128)S(1)} %copy-done), kind=kOutput, calls=%fused_computation.32 | convolution fusion | flops 51380224 | bytes 8392709 | tf_op jit(solution)/shard_map/pq,...qb->...pb/dot_general | solution.py:26
  79.1 2.1 fusion.27
  81.2 2.2 fusion.12
  83.5 3.9 %bitcast_dynamic-update-slice_fusion.1 = f32[1,2,4,64,8,512]{5,4,3,2,1,0:T(8,128)} fusion(f32[1,2,4,64,8,512]{5,4,3,2,1,0:T(8,128)} %bitcast_dynamic-update-slice_fusion.2, s32[]{:T(128)S(6)} %select_n.129, f32[2,64,512,8]{2,3,1,0:T(8,128)S(1)} %fusion.8, bf16[1,2,64,8,512]{4,3,2,1,0:T(8,128)(2,1)S(1)} %collective-permute-done.1, ...), kind=kOutput, calls=%fused_computation.26 | convolution fusion | flops 52428800 | bytes 9441285 | tf_op jit(solution)/shard_map/pq,...qb->...pb/dot_general | solution.py:26
  87.4 3.9 %bitcast_dynamic-update-slice_fusion = f32[1,2,4,64,8,512]{5,4,3,2,1,0:T(8,128)} fusion(f32[1,2,4,64,8,512]{5,4,3,2,1,0:T(8,128)} %bitcast_dynamic-update-slice_fusion.1, s32[]{:T(128)S(6)} %select_n.137, f32[2,64,512,8]{2,3,1,0:T(8,128)S(1)} %fusion.12, bf16[1,2,64,8,512]{4,3,2,1,0:T(8,128)(2,1)S(1)} %collective-permute-done.2, ...), kind=kOutput, calls=%fused_computation.20 | convolution fusion | flops 52428800 | bytes 9441285 | tf_op jit(solution)/shard_map/pq,...qb->...pb/dot_general | solution.py:26
  91.3 5.3 %conditional.7 = (f32[1,1,256,8,512]{4,3,2,1,0:T(8,128)}) conditional(s32[]{:T(128)} %clamp.9, f32[1,2,4,64,8,512]{5,4,3,2,1,0:T(8,128)} %bitcast_dynamic-update-slice_fusion, f32[1,2,4,64,8,512]{5,4,3,2,1,0:T(8,128)} %bitcast_dynamic-update-slice_fusion, ...), branch_computations={%region_14.15_spmd, %region_15.16_spmd, %region_16.17_spmd, %regio... | conditional | bytes 16777224 | solution.py:57
  91.3 2.6 %slice.143 = f32[1,1,4,64,8,512]{5,4,3,2,1,0:T(8,128)S(1)} slice(f32[1,2,4,64,8,512]{5,4,3,2,1,0:T(8,128)} %param.13), slice={[0:1], [1:2], [0:4], [0:64], [0:8], [0:512]} | slice | bytes 8388608 | tf_op jit(solution)/shard_map/slice | solution.py:106
  93.9 2.5 copy.120
  96.6 5.2 %conditional.6 = (f32[1,1,256,8,512]{4,3,2,1,0:T(8,128)}) conditional(s32[]{:T(128)} %clamp.8, f32[1,2,4,64,8,512]{5,4,3,2,1,0:T(8,128)} %bitcast_dynamic-update-slice_fusion, f32[1,2,4,64,8,512]{5,4,3,2,1,0:T(8,128)} %bitcast_dynamic-update-slice_fusion, ...), branch_computations={%region_10.11_spmd, %region_11.12_spmd, %region_12.13_spmd, %regio... | conditional | bytes 16777224 | solution.py:57
  96.6 2.6 %slice.138 = f32[1,1,4,64,8,512]{5,4,3,2,1,0:T(8,128)S(1)} slice(f32[1,2,4,64,8,512]{5,4,3,2,1,0:T(8,128)} %param.8), slice={[0:1], [0:1], [0:4], [0:64], [0:8], [0:512]} | slice | bytes 8388608 | tf_op jit(solution)/shard_map/slice | solution.py:106
  99.2 2.6 %copy.116 = f32[1,4,4,4,4,8,512]{6,5,1,4,3,2,0:T(8,128)} copy(f32[1,4,4,4,4,8,512]{6,5,4,3,2,1,0:T(8,128)S(1)} %bitcast.307) | data formatting | bytes 8388608 | tf_op jit(solution)/shard_map/reshape;squeeze | solution.py:106
  101.8 7.9 %pad_maximum_fusion = f32[1,2,256,8,512]{4,3,1,0,2:T(8,128)} fusion(f32[1,1,256,8,512]{4,3,1,0,2:T(8,128)} %bitcast.314, f32[1,1,256,8,512]{4,3,1,0,2:T(8,128)} %bitcast.319), kind=kLoop, calls=%fused_computation | loop fusion | flops 2097152 | bytes 16777216 | tf_op jit(solution)/shard_map/stack | solution.py:110
  109.8 5.2 %all-to-all-start = ((f32[1,2,256,8,512]{4,3,1,0,2:T(8,128)}), f32[1,2,256,8,512]{4,3,1,0,2:T(8,128)}, u32[]{:S(2)}, u32[]{:S(2)}) async-start(f32[1,2,256,8,512]{4,3,1,0,2:T(8,128)} %pad_maximum_fusion), calls=%async_computation | async-start | bytes 16777216 | tf_op jit(solution)/shard_map/all_to_all | solution.py:117
  115.1 93.8 %all-to-all-done = f32[1,2,256,8,512]{4,3,1,0,2:T(8,128)} async-done(((f32[1,2,256,8,512]{4,3,1,0,2:T(8,128)}), f32[1,2,256,8,512]{4,3,1,0,2:T(8,128)}, u32[]{:S(2)}, u32[]{:S(2)}) %all-to-all-start) | async-done | bytes 8388640 | tf_op jit(solution)/shard_map/all_to_all | solution.py:117
  209.0 15.4 %copy.153 = f32[1,2,8,32,8,512]{5,1,2,4,3,0:T(2,128)} copy(f32[1,2,8,32,8,512]{5,4,1,3,2,0:T(8,128)} %bitcast.127) | data formatting | bytes 16777216 | tf_op jit(solution)/shard_map/all_to_all | solution.py:117
  224.4 10.9 %reshape.144 = f32[16,32,8,512,1]{3,0,2,1,4:T(8,128)} reshape(f32[1,8,2,32,8,512]{5,2,1,4,3,0:T(2,128)} %bitcast.303) | data formatting | bytes 16777216 | tf_op jit(solution)/shard_map/reshape.26
  235.2 8.9 %fusion.26 = (f32[32,4]{1,0:T(8,128)S(1)}, f32[32,512,4,8,1]{1,3,4,2,0:T(8,128)}) fusion(f32[4,4,8,8]{1,2,3,0:T(8,128)S(1)} %broadcast_multiply_fusion.1, f32[4,12,8,8]{1,2,3,0:T(8,128)S(1)} %copy_negate_fusion, f32[16,32,8,512,1]{3,0,2,1,4:T(8,128)} %reshape.144), kind=kOutput, calls=%fused_computation.39 | convolution fusion | flops 806358912 | bytes 10502656 | tf_op jit(solution)/shard_map/ijpq,sjlqb->lsipb/dot_general | solution.py:114
  244.2 12.1 %psum.7 = f32[32,4]{0,1:T(4,128)S(1)} all-reduce(f32[32,4]{0,1:T(4,128)S(1)} %broadcast_multiply_fusion.2), channel_id=1, replica_groups=mesh['node'=8,'stripe'=4] {'stripe'}, use_global_device_ids=true, to_apply=%region_19.20 | all-reduce | flops 128 | bytes 1024 | tf_op jit(solution)/shard_map/psum | solution.py:121
  256.4 0.6 fusion.72
  (24 shorter events, 0.5 us)
Async XLA Ops:
  0.6 26.5 %copy-start = (f32[8,8]{1,0:T(8,128)S(1)}, f32[8,8]{1,0:T(8,128)}, u32[]{:S(2)}) copy-start(f32[8,8]{1,0:T(8,128)} %param.20) | copy-start | bytes 772
  3.3 2.0 copy-start.3
  6.0 1.3 copy-start.4
  20.8 40.4 %collective-permute-start = (bf16[1,2,64,8,512]{4,3,2,1,0:T(8,128)(2,1)}, bf16[1,2,64,8,512]{4,3,2,1,0:T(8,128)(2,1)S(1)}, u32[]{:S(2)}, u32[]{:S(2)}) collective-permute-start(bf16[1,2,64,8,512]{4,3,2,1,0:T(8,128)(2,1)} %get-tuple-element.98), channel_id=1, source_target_pairs={{24,0},{28,4},{0,8},{4,12},{8,16},{12,20},{16,24},{20,28},{25,1},{... | collective-permute-start | bytes 3145736 | tf_op jit(solution)/shard_map/ppermute | solution.py:22
  23.8 47.0 %collective-permute-start.1 = (bf16[1,2,64,8,512]{4,3,2,1,0:T(8,128)(2,1)}, bf16[1,2,64,8,512]{4,3,2,1,0:T(8,128)(2,1)S(1)}, u32[]{:S(2)}, u32[]{:S(2)}) collective-permute-start(bf16[1,2,64,8,512]{4,3,2,1,0:T(8,128)(2,1)} %get-tuple-element.97), channel_id=1, source_target_pairs={{16,0},{20,4},{24,8},{28,12},{0,16},{4,20},{8,24},{12,28},{17,1},{... | collective-permute-start | bytes 3145736 | tf_op jit(solution)/shard_map/ppermute | solution.py:22
  25.3 53.8 %collective-permute-start.2 = (bf16[1,2,64,8,512]{4,3,2,1,0:T(8,128)(2,1)}, bf16[1,2,64,8,512]{4,3,2,1,0:T(8,128)(2,1)S(1)}, u32[]{:S(2)}, u32[]{:S(2)}) collective-permute-start(bf16[1,2,64,8,512]{4,3,2,1,0:T(8,128)(2,1)} %get-tuple-element.96), channel_id=1, source_target_pairs={{8,0},{12,4},{16,8},{20,12},{24,16},{28,20},{0,24},{4,28},{9,1},{1... | collective-permute-start | bytes 3145736 | tf_op jit(solution)/shard_map/ppermute | solution.py:22
  61.2 4.1 %copy-start.2 = (f32[1,2,4,64,8,512]{5,4,3,2,1,0:T(8,128)S(1)}, f32[1,2,4,64,8,512]{5,4,3,2,1,0:T(8,128)}, u32[]{:S(2)}) copy-start(f32[1,2,4,64,8,512]{5,4,3,2,1,0:T(8,128)} %get-tuple-element.100) | copy-start | bytes 25165828
  109.8 5.3 %copy-start.5 = (f32[4,12,8,8]{1,3,2,0:T(8,128)S(1)}, f32[4,12,8,8]{1,3,2,0:T(8,128)}, u32[]{:S(2)}) copy-start(f32[4,12,8,8]{1,3,2,0:T(8,128)} %param.21) | copy-start | bytes 36868
  109.8 99.2 %all-to-all-start = ((f32[1,2,256,8,512]{4,3,1,0,2:T(8,128)}), f32[1,2,256,8,512]{4,3,1,0,2:T(8,128)}, u32[]{:S(2)}, u32[]{:S(2)}) async-start(f32[1,2,256,8,512]{4,3,1,0,2:T(8,128)} %pad_maximum_fusion), calls=%async_computation | async-start | bytes 16777216 | tf_op jit(solution)/shard_map/all_to_all | solution.py:117
  235.2 21.7 %copy-start.1 = (f32[8,8]{1,0:T(8,128)S(1)}, f32[8,8]{1,0:T(8,128)}, u32[]{:S(2)}) copy-start(f32[8,8]{1,0:T(8,128)} %param.20) | copy-start | bytes 772
where the time goes:
time: 261 us; the launch traced here: 257 us
  waiting for transfers between devices  97 us (37%)
  local copies, waits for them, and re-layouts  56.5 us (22%)
  other arithmetic  44.5 us (17%)
  matrix products  34 us (13%)
  blocking collectives  12.1 us (5%)
  starting transfers between devices  11.5 us (4%)
    all_to_all x1, waiting for transfers between devices, local(): lax.all_to_all(uncoupled, 'node', split_axis=2, concat_axis=1, tiled=True)  93.8 us
    dot_general x9, matrix products, mix_planes(): return jnp.einsum('pq,...qb->...pb', matrix, values, precision=precise)  24.7 us
    div x1, other arithmetic, inverse_factor(): solved_rows.append(running / factor[row_at, row_at])  22.5 us
    all_to_all x1, local copies, waits for them, and re-layouts, local(): lax.all_to_all(uncoupled, 'node', split_axis=2, concat_axis=1, tiled=True)  15.4 us
    psum x1, blocking collectives, local(): pool_sum = lax.psum(jnp.sum(energy, axis=1), 'stripe')  12.1 us
    unnamed x13, local copies, waits for them, and re-layouts  11 us
    another operation x1, local copies, waits for them, and re-layouts  10.9 us
    dot_general x1, matrix products, local(): jnp.einsum('ijpq,sjlqb->lsipb', weights_all, lax.all_to_all(uncoupled, 'n...  8.93 us
  transfers between devices with their start and end apart: 4, of which 2 were waited for; matrix products, arithmetic and copies ran while one was open for 19% of the time, Pallas kernels for 0%

commit v1 on v0

--- a/solution.py
+++ b/solution.py
@@ -10,6 +10,13 @@
 VIRTUAL = 2
 precise = lax.Precision.HIGHEST
 epsilon = 1e-06
+
+
+def exchange_blocks(x, name, split, join):
+    count = lax.axis_size(name)
+    pieces = jnp.stack(jnp.split(x, count, axis=split), axis=0)
+    pieces = lax.all_to_all(pieces, name, split_axis=0, concat_axis=0)
+    return jnp.concatenate(pieces, axis=join)
 
 
 def for_sending(x):
@@ -114,7 +121,7 @@
     syndrome = jnp.einsum(
         "ijpq,sjlqb->lsipb",
         weights_all,
-        lax.all_to_all(uncoupled, "node", split_axis=2, concat_axis=1, tiled=True),
+        exchange_blocks(uncoupled, "node", 2, 1),
         precision=precise,
     )
     energy = jnp.mean(syndrome * syndrome, axis=(3, 4))

time: 261 us -> 241 us (0.923)
  local copies, waits for them, and re-layouts: 56.5 us -> 32.9 us
    all_to_all x1 -> x0, local copies, waits for them, and re-layouts: 15.4 us -> none  [local(): lax.all_to_all(uncoupled, 'node', split_axis=2, concat_axis=1, tiled=True)]
    another operation x1 -> x0, local copies, waits for them, and re-layouts: 10.9 us -> none
    unnamed x0 -> x8, other arithmetic: none -> 8.71 us
    another operation x1, other arithmetic: 7.92 us -> 1.12 us  [exchange_blocks(): pieces = jnp.stack(jnp.split(x, count, axis=split), axis=0)]
    dot_general x1, matrix products: 8.93 us -> 14.9 us  [local(): jnp.einsum('ijpq,sjlqb->lsipb', weights_all, exchange_blocks(uncoupled, '...]
    unnamed x13 -> x23, local copies, waits for them, and re-layouts: 11 us -> 15.8 us
    dot_general x9, matrix products: 24.7 us -> 20.3 us  [mix_planes(): return jnp.einsum('pq,...qb->...pb', matrix, values, precision=precise)]
  transfers between devices with their start and end apart: 4 -> 4, of which waited for: 2 -> 2; matrix products, arithmetic and copies ran while one was open for 19% -> 20% of each run, Pallas kernels for 0% -> 0%
where the time goes in v1:
time: 241 us; the launch traced here: 237 us
  waiting for transfers between devices  96.8 us (40%)
  other arithmetic  46.6 us (19%)
  matrix products  35.6 us (15%)
  local copies, waits for them, and re-layouts  32.9 us (14%)
  blocking collectives  12.1 us (5%)
  starting transfers between devices  11.5 us (5%)
    all_to_all x1, waiting for transfers between devices, exchange_blocks(): pieces = lax.all_to_all(pieces, name, split_axis=0, concat_axis=0)  93.8 us
    div x1, other arithmetic, inverse_factor(): solved_rows.append(running / factor[row_at, row_at])  22.5 us
    dot_general x9, matrix products, mix_planes(): return jnp.einsum('pq,...qb->...pb', matrix, values, precision=precise)  20.3 us
    unnamed x23, local copies, waits for them, and re-layouts  15.8 us
    dot_general x1, matrix products, local(): jnp.einsum('ijpq,sjlqb->lsipb', weights_all, exchange_blocks(uncoupled, '...  14.9 us
    psum x1, blocking collectives, local(): pool_sum = lax.psum(jnp.sum(energy, axis=1), 'stripe')  12.1 us
    unnamed x8, other arithmetic  8.71 us
    another operation x1, other arithmetic, local(): fronted = jnp.stack(fronts, axis=1)  6.73 us
  transfers between devices with their start and end apart: 4, of which 2 were waited for; matrix products, arithmetic and copies ran while one was open for 20% of the time, Pallas kernels for 0%

profile of v1, /device:TPU:0, one launch (start us, length us, event | category | flops | bytes accessed | tf_op | source)
XLA Modules:
  0.0 237.1 jit_solution(16338722474759037614)
XLA Ops:
  0.8 2.5 %broadcast_multiply_fusion = bf16[1,2,256,8,512]{4,3,2,1,0:T(8,128)(2,1)S(1)} fusion(bf16[1,2,256,8,512]{4,3,2,1,0:T(8,128)(2,1)} %param.19, bf16[2]{0:T(256)(128)(2,1)S(1)} %or_convert_fusion), kind=kLoop, calls=%fused_computation.61 | loop fusion | flops 2097152 | bytes 8388612 | tf_op jit(solution)/shard_map/mul | solution.py:77
  3.3 1.9 copy-done.6
  5.2 0.7 conditional.5
  6.0 1.3 copy-done.7
  7.3 3.1 %conditional.4 = (bf16[1,1,4,64,8,512]{5,4,2,3,1,0:T(8,128)(2,1)}) conditional(s32[]{:T(128)} %clamp.8, bf16[1,2,256,8,512]{4,3,2,1,0:T(8,128)(2,1)} %copy-done.6, bf16[1,2,256,8,512]{4,3,2,1,0:T(8,128)(2,1)} %copy-done.6, bf16[1,2,256,8,512]{4,3,2,1,0:T(8,128)(2,1)} %copy-done.6, ...), branch_computations={%region_0.1_spmd, %region_1.2_spmd, %region_2.3_spmd, %region_3.4_... | conditional | bytes 14680096 | solution.py:56
  7.3 3.0 %slice.130 = bf16[1,1,256,8,512]{4,3,2,1,0:T(8,128)(2,1)} slice(bf16[1,2,256,8,512]{4,3,2,1,0:T(8,128)(2,1)} %param), slice={[0:1], [0:1], [0:256], [0:8], [0:512]} | slice | bytes 4194304 | tf_op jit(solution)/shard_map/slice | solution.py:81
  10.3 6.7 %fusion.98 = (bf16[1,2,4,64,8,512]{5,4,3,2,1,0:T(8,128)(2,1)}, f32[1,2,4,64,8,512]{5,4,3,2,1,0:T(8,128)}) fusion(bf16[1,1,4,64,8,512]{5,4,2,3,1,0:T(8,128)(2,1)} %copy-done.7, bf16[1,1,4,64,8,512]{5,4,2,3,1,0:T(8,128)(2,1)} %get-tuple-element.139), kind=kLoop, calls=%fused_computation.140 | loop fusion | flops 4194304 | bytes 16777216 | tf_op jit(solution)/shard_map/stack | solution.py:87
  17.1 3.6 %dynamic-slice_bitcast_fusion = (bf16[1,2,64,8,512]{4,3,2,1,0:T(8,128)(2,1)}, bf16[1,2,64,8,512]{4,3,2,1,0:T(8,128)(2,1)}, bf16[1,2,64,8,512]{4,3,2,1,0:T(8,128)(2,1)}) fusion(bf16[1,2,4,64,8,512]{5,4,3,2,1,0:T(8,128)(2,1)} %get-tuple-element.99, s32[]{:T(128)S(6)} %select_n.139, s32[]{:T(128)S(6)} %select_n.131, s32[]{:T(128)S(6)} %select_n.122), kind=kLoop, calls=%fused_computation.90 | loop fusion | bytes 6291468 | tf_op jit(solution)/shard_map/jit(dynamic_index_in_dim)/squeeze | solution.py:93
  20.6 3.0 %collective-permute-start = (bf16[1,2,64,8,512]{4,3,2,1,0:T(8,128)(2,1)}, bf16[1,2,64,8,512]{4,3,2,1,0:T(8,128)(2,1)S(1)}, u32[]{:S(2)}, u32[]{:S(2)}) collective-permute-start(bf16[1,2,64,8,512]{4,3,2,1,0:T(8,128)(2,1)} %get-tuple-element.98), channel_id=1, source_target_pairs={{24,0},{28,4},{0,8},{4,12},{8,16},{12,20},{16,24},{20,28},{25,1},{... | collective-permute-start | bytes 3145736 | tf_op jit(solution)/shard_map/ppermute | solution.py:29
  23.6 1.5 collective-permute-start.1
  25.1 1.9 collective-permute-start.2
  27.3 0.7 cholesky.14
  28.1 7.6 %copy.163 = f32[1,2,4,64,8,512]{5,4,3,2,1,0:T(8,128)} copy(f32[1,2,4,64,8,512]{5,4,3,2,1,0:T(8,128)} %get-tuple-element.100) | data formatting | bytes 16777216
  35.7 0.7 compare_reduce_fusion
  36.4 0.7 select_select_fusion
  37.1 0.7 fusion.100
  37.8 0.7 fusion.99
  38.5 22.5 %subtract_divide_fusion = (f32[1,8]{1,0:T(1,128)S(1)}, f32[1,8]{1,0:T(1,128)S(1)}, f32[1,8]{1,0:T(1,128)S(1)}, f32[1,8]{1,0:T(1,128)S(1)}, f32[1,8]{1,0:T(1,128)...) fusion(f32[8,8]{1,0:T(8,128)S(1)} %fusion.89, f32[]{:T(128)} %bitcast.83, f32[]{:T(128)} %bitcast.82, ...), kind=kLoop, calls=%fused_computation.130 | loop fusion | flops 512 | bytes 656 | tf_op jit(solution)/shard_map/div | solution.py:46
  61.3 2.1 convert_select_fusion.5
  63.4 2.0 fusion.33
  65.4 2.2 fusion.4
  67.6 2.9 %collective-permute-done.1 = bf16[1,2,64,8,512]{4,3,2,1,0:T(8,128)(2,1)S(1)} collective-permute-done((bf16[1,2,64,8,512]{4,3,2,1,0:T(8,128)(2,1)}, bf16[1,2,64,8,512]{4,3,2,1,0:T(8,128)(2,1)S(1)}, u32[]{:S(2)}, u32[]{:S(2)}) %collective-permute-start.1) | collective-permute-done | bytes 1048608 | tf_op jit(solution)/shard_map/ppermute | solution.py:29
  70.6 2.1 fusion.30
  72.7 2.2 fusion.8
  74.9 2.5 %bitcast_dynamic-update-slice_fusion.2 = f32[1,2,4,64,8,512]{5,4,3,2,1,0:T(8,128)S(1)} fusion(f32[1,2,4,64,8,512]{5,4,3,2,1,0:T(8,128)S(1)} %bitcast.331, s32[]{:T(128)S(6)} %select_n.120, f32[1,2,64,8,512]{4,3,2,1,0:T(8,128)S(1)} %convert_select_fusion.5, f32[2,64,512,8]{2,3,1,0:T(8,128)S(1)} %fusion.4, pred[]{:T(512)S(6)} %lt.82, f32[8,8]{1,0:T(8,128)S(1)} %copy-done), kind=kOutput, calls=%fused_computation.44 | convolution fusion | flops 51380224 | bytes 8392709 | tf_op jit(solution)/shard_map/pq,...qb->...pb/dot_general | solution.py:33
  77.5 2.1 fusion.27
  79.6 2.2 fusion.12
  81.9 2.5 %bitcast_dynamic-update-slice_fusion.1 = f32[1,2,4,64,8,512]{5,4,3,2,1,0:T(8,128)S(1)} fusion(f32[1,2,4,64,8,512]{5,4,3,2,1,0:T(8,128)S(1)} %bitcast_dynamic-update-slice_fusion.2, s32[]{:T(128)S(6)} %select_n.129, f32[2,64,512,8]{2,3,1,0:T(8,128)S(1)} %fusion.8, bf16[1,2,64,8,512]{4,3,2,1,0:T(8,128)(2,1)S(1)} %collective-permute-done.1, ...), kind=kOutput, calls=%fused_computation.38 | convolution fusion | flops 52428800 | bytes 9441285 | tf_op jit(solution)/shard_map/pq,...qb->...pb/dot_general | solution.py:33
  84.3 2.5 %bitcast_dynamic-update-slice_fusion = f32[1,2,4,64,8,512]{5,4,3,2,1,0:T(8,128)S(1)} fusion(f32[1,2,4,64,8,512]{5,4,3,2,1,0:T(8,128)S(1)} %bitcast_dynamic-update-slice_fusion.1, s32[]{:T(128)S(6)} %select_n.137, f32[2,64,512,8]{2,3,1,0:T(8,128)S(1)} %fusion.12, bf16[1,2,64,8,512]{4,3,2,1,0:T(8,128)(2,1)S(1)} %collective-permute-done.2, ...), kind=kOutput, calls=%fused_computation.32 | convolution fusion | flops 52428800 | bytes 9441285 | tf_op jit(solution)/shard_map/pq,...qb->...pb/dot_general | solution.py:33
  86.8 3.2 %copy-done.4 = f32[1,2,4,64,8,512]{5,4,3,2,1,0:T(8,128)} copy-done((f32[1,2,4,64,8,512]{5,4,3,2,1,0:T(8,128)}, f32[1,2,4,64,8,512]{5,4,3,2,1,0:T(8,128)S(1)}, u32[]{:S(2)}) %copy-start.4) | copy-done | bytes 8388632
  90.1 3.3 %conditional.6 = (f32[1,1,256,8,512]{4,3,2,1,0:T(8,128)}) conditional(s32[]{:T(128)} %clamp.8, f32[1,2,4,64,8,512]{5,4,3,2,1,0:T(8,128)S(1)} %bitcast_dynamic-update-slice_fusion, f32[1,2,4,64,8,512]{5,4,3,2,1,0:T(8,128)S(1)} %bitcast_dynamic-update-slice_fusion, ...), branch_computations={%region_10.11_spmd, %region_11.12_spmd, %region_12.13_spmd, %regio... | conditional | bytes 16777224 | solution.py:64
  90.5 2.6 %copy.114 = f32[1,4,4,4,4,8,512]{6,5,1,4,3,2,0:T(8,128)} copy(f32[1,4,4,4,4,8,512]{6,5,4,3,2,1,0:T(8,128)S(1)} %bitcast.335) | data formatting | bytes 8388608 | tf_op jit(solution)/shard_map/reshape;squeeze | solution.py:113
  93.3 5.1 %conditional.7 = (f32[1,1,256,8,512]{4,3,2,1,0:T(8,128)}) conditional(s32[]{:T(128)} %clamp.9, f32[1,2,4,64,8,512]{5,4,3,2,1,0:T(8,128)} %copy-done.4, f32[1,2,4,64,8,512]{5,4,3,2,1,0:T(8,128)} %copy-done.4, f32[1,2,4,64,8,512]{5,4,3,2,1,0:T(8,128)} %copy-done.4, f32[1,2,4,64,8,512]{5,4,3,2,1,0:T(8,128)} %copy-done.4), branch_computations={%region_14.15_spmd, %region_15.16_spmd, %region_16.17_spmd, %regio... | conditional | bytes 16777224 | solution.py:64
  93.4 2.6 %slice.143 = f32[1,1,4,64,8,512]{5,4,3,2,1,0:T(8,128)S(1)} slice(f32[1,2,4,64,8,512]{5,4,3,2,1,0:T(8,128)} %param.13), slice={[0:1], [1:2], [0:4], [0:64], [0:8], [0:512]} | slice | bytes 8388608 | tf_op jit(solution)/shard_map/slice | solution.py:113
  96.0 2.4 %copy.118 = f32[1,4,4,4,4,8,512]{6,5,4,1,3,2,0:T(8,128)} copy(f32[1,4,4,4,4,8,512]{6,5,4,3,2,1,0:T(8,128)S(1)} %bitcast.339) | data formatting | bytes 8388608 | tf_op jit(solution)/shard_map/reshape;squeeze | solution.py:113
  98.4 2.4 %fusion.44 = f32[8,1,2,32,8,512]{5,4,3,2,1,0:T(8,128)} fusion(f32[1,1,256,8,512]{4,3,2,1,0:T(8,128)} %get-tuple-element.141, f32[1,1,256,8,512]{4,3,2,1,0:T(8,128)} %get-tuple-element.142), kind=kLoop, calls=%fused_computation.71 | loop fusion | flops 262143 | bytes 9437184
  101.3 1.3 copy-done.3
  102.6 1.0 fusion.47
  103.6 1.1 fusion.50
  104.7 1.0 fusion.53
  105.7 1.1 fusion.56
  106.8 1.1 fusion.59
  107.9 1.0 fusion.41
  108.9 1.1 fusion.61
  110.0 5.2 %all-to-all-start = ((f32[8,1,2,32,8,512]{5,4,3,2,1,0:T(8,128)}), f32[8,1,2,32,8,512]{5,4,3,2,1,0:T(8,128)}, u32[]{:S(2)}, u32[]{:S(2)}) async-start(f32[8,1,2,32,8,512]{5,4,3,2,1,0:T(8,128)} %fusion.61), calls=%async_computation | async-start | bytes 16777216 | tf_op jit(solution)/shard_map/all_to_all | solution.py:18
  115.4 93.8 %all-to-all-done = f32[8,1,2,32,8,512]{5,4,3,2,1,0:T(8,128)} async-done(((f32[8,1,2,32,8,512]{5,4,3,2,1,0:T(8,128)}), f32[8,1,2,32,8,512]{5,4,3,2,1,0:T(8,128)}, u32[]{:S(2)}, u32[]{:S(2)}) %all-to-all-start) | async-done | bytes 8388640 | tf_op jit(solution)/shard_map/all_to_all | solution.py:18
  209.2 14.9 %fusion.26 = (f32[32,4]{1,0:T(8,128)S(1)}, f32[32,512,4,8,1]{1,3,4,2,0:T(8,128)}) fusion(f32[4,4,8,8]{1,2,3,0:T(8,128)S(1)} %broadcast_multiply_fusion.1, f32[4,12,8,8]{1,2,3,0:T(8,128)S(1)} %copy_negate_fusion, f32[16,32,8,512,1]{3,2,1,0,4:T(8,128)} %bitcast.134), kind=kOutput, calls=%fused_computation.51 | convolution fusion | flops 806358912 | bytes 10502656 | tf_op jit(solution)/shard_map/ijpq,sjlqb->lsipb/dot_general | solution.py:121
  224.2 12.1 %psum.7 = f32[32,4]{0,1:T(4,128)S(1)} all-reduce(f32[32,4]{0,1:T(4,128)S(1)} %broadcast_multiply_fusion.2), channel_id=1, replica_groups=mesh['node'=8,'stripe'=4] {'stripe'}, use_global_device_ids=true, to_apply=%region_19.20 | all-reduce | flops 128 | bytes 1024 | tf_op jit(solution)/shard_map/psum | solution.py:128
  (40 shorter events, 3.0 us)
Async XLA Ops:
  0.6 26.4 %copy-start = (f32[8,8]{1,0:T(8,128)S(1)}, f32[8,8]{1,0:T(8,128)}, u32[]{:S(2)}) copy-start(f32[8,8]{1,0:T(8,128)} %param.20) | copy-start | bytes 772
  3.3 1.9 copy-start.6
  5.9 1.3 copy-start.7
  20.6 40.6 %collective-permute-start = (bf16[1,2,64,8,512]{4,3,2,1,0:T(8,128)(2,1)}, bf16[1,2,64,8,512]{4,3,2,1,0:T(8,128)(2,1)S(1)}, u32[]{:S(2)}, u32[]{:S(2)}) collective-permute-start(bf16[1,2,64,8,512]{4,3,2,1,0:T(8,128)(2,1)} %get-tuple-element.98), channel_id=1, source_target_pairs={{24,0},{28,4},{0,8},{4,12},{8,16},{12,20},{16,24},{20,28},{25,1},{... | collective-permute-start | bytes 3145736 | tf_op jit(solution)/shard_map/ppermute | solution.py:29
  23.6 47.0 %collective-permute-start.1 = (bf16[1,2,64,8,512]{4,3,2,1,0:T(8,128)(2,1)}, bf16[1,2,64,8,512]{4,3,2,1,0:T(8,128)(2,1)S(1)}, u32[]{:S(2)}, u32[]{:S(2)}) collective-permute-start(bf16[1,2,64,8,512]{4,3,2,1,0:T(8,128)(2,1)} %get-tuple-element.97), channel_id=1, source_target_pairs={{16,0},{20,4},{24,8},{28,12},{0,16},{4,20},{8,24},{12,28},{17,1},{... | collective-permute-start | bytes 3145736 | tf_op jit(solution)/shard_map/ppermute | solution.py:29
  25.1 52.4 %collective-permute-start.2 = (bf16[1,2,64,8,512]{4,3,2,1,0:T(8,128)(2,1)}, bf16[1,2,64,8,512]{4,3,2,1,0:T(8,128)(2,1)S(1)}, u32[]{:S(2)}, u32[]{:S(2)}) collective-permute-start(bf16[1,2,64,8,512]{4,3,2,1,0:T(8,128)(2,1)} %get-tuple-element.96), channel_id=1, source_target_pairs={{8,0},{12,4},{16,8},{20,12},{24,16},{28,20},{0,24},{4,28},{9,1},{1... | collective-permute-start | bytes 3145736 | tf_op jit(solution)/shard_map/ppermute | solution.py:29
  61.3 4.1 %copy-start.5 = (f32[1,2,4,64,8,512]{5,4,3,2,1,0:T(8,128)S(1)}, f32[1,2,4,64,8,512]{5,4,3,2,1,0:T(8,128)}, u32[]{:S(2)}) copy-start(f32[1,2,4,64,8,512]{5,4,3,2,1,0:T(8,128)} %get-tuple-element.100) | copy-start | bytes 25165828
  65.4 9.5 %slice-start = ((s8[8388608]{0:T(1024)(128)(4,1)}), s8[4194304]{0:T(1024)(128)(4,1)S(1)}, s32[]{:S(2)}) async-start(s8[8388608]{0:T(1024)(128)(4,1)} %bitcast.330), calls=%async_computation.1 | async-start | bytes 8388608
  67.6 7.3 %slice-start.1 = ((s8[8388608]{0:T(1024)(128)(4,1)}), s8[4194304]{0:T(1024)(128)(4,1)S(1)}, s32[]{:S(2)}) async-start(s8[8388608]{0:T(1024)(128)(4,1)} %bitcast.330), calls=%async_computation.2 | async-start | bytes 8388608
  86.8 3.3 %copy-start.4 = (f32[1,2,4,64,8,512]{5,4,3,2,1,0:T(8,128)}, f32[1,2,4,64,8,512]{5,4,3,2,1,0:T(8,128)S(1)}, u32[]{:S(2)}) copy-start(f32[1,2,4,64,8,512]{5,4,3,2,1,0:T(8,128)S(1)} %bitcast_dynamic-update-slice_fusion) | copy-start | bytes 25165828
  98.4 2.9 %copy-start.2 = (f32[1,1,256,8,512]{4,3,2,1,0:T(8,128)S(1)}, f32[1,1,256,8,512]{4,3,2,1,0:T(8,128)}, u32[]{:S(2)}) copy-start(f32[1,1,256,8,512]{4,3,2,1,0:T(8,128)} %get-tuple-element.141) | copy-start | bytes 12582916
  98.4 4.2 %copy-start.3 = (f32[1,1,256,8,512]{4,3,2,1,0:T(8,128)S(1)}, f32[1,1,256,8,512]{4,3,2,1,0:T(8,128)}, u32[]{:S(2)}) copy-start(f32[1,1,256,8,512]{4,3,2,1,0:T(8,128)} %get-tuple-element.142) | copy-start | bytes 12582916
  110.0 5.3 %copy-start.8 = (f32[4,12,8,8]{1,3,2,0:T(8,128)S(1)}, f32[4,12,8,8]{1,3,2,0:T(8,128)}, u32[]{:S(2)}) copy-start(f32[4,12,8,8]{1,3,2,0:T(8,128)} %param.21) | copy-start | bytes 36868
  110.0 99.2 %all-to-all-start = ((f32[8,1,2,32,8,512]{5,4,3,2,1,0:T(8,128)}), f32[8,1,2,32,8,512]{5,4,3,2,1,0:T(8,128)}, u32[]{:S(2)}, u32[]{:S(2)}) async-start(f32[8,1,2,32,8,512]{5,4,3,2,1,0:T(8,128)} %fusion.61), calls=%async_computation | async-start | bytes 16777216 | tf_op jit(solution)/shard_map/all_to_all | solution.py:18
  209.2 27.7 %copy-start.1 = (f32[8,8]{1,0:T(8,128)S(1)}, f32[8,8]{1,0:T(8,128)}, u32[]{:S(2)}) copy-start(f32[8,8]{1,0:T(8,128)} %param.20) | copy-start | bytes 772
